TPU v7x, 32 devices: a whole 2x2x4 slice. The times are simulated.
32 devices in a mesh: dp: 4 (over x, y), tp: 8 (over z, core).
Axes of the slice: x: 2, y: 2, z: 4, core: 2. Of those that a mesh axis runs over, the one named last changes fastest.
Arguments:
- x: bfloat16 [8192, 7168], P('dp'), parts along dimension 0
- w_gate: bfloat16 [7168, 20480], P(None, 'tp')
- w_up: bfloat16 [7168, 20480], P(None, 'tp')
- w_down: bfloat16 [20480, 7168], P('tp')
Outputs:
- output: bfloat16 [8192, 7168], P('dp'), parts along dimension 0
There are 4 independent parts. A program takes and returns all parts, laid end to end along the dimension named above; an argument that names none is the same for every part.
All inputs are finite; a program needn't handle non-finite values.
Results may differ from a plain program's by a relative error of at most 0.016.
Values are sent between devices in bfloat16 or wider.
A program may use at most 2 GiB of HBM per device.

v0:
```python
import jax
import jax.numpy as jnp
from jax import lax
from jax.sharding import PartitionSpec as P


def solution(mesh):
    def step(x, w_gate, w_up, w_down):
        gate = jnp.dot(x, w_gate, preferred_element_type=jnp.float32)
        up = jnp.dot(x, w_up, preferred_element_type=jnp.float32)
        hidden = (jax.nn.silu(gate) * up).astype(jnp.bfloat16)
        term = jnp.dot(hidden, w_down, preferred_element_type=jnp.float32).astype(jnp.bfloat16)
        return lax.psum(term, "tp")

    return jax.shard_map(
        step,
        mesh=mesh,
        in_specs=(P("dp", None), P(None, "tp"), P(None, "tp"), P("tp", None)),
        out_specs=P("dp", None),
        check_vma=False,
    )
```

profile of v0, /device:TPU:0, one launch (start us, length us, event | category | flops | bytes accessed | tf_op | source)
XLA Modules:
  0.0 867.6 jit_solution(13627236918569953072)
XLA Ops:
  6.5 0.0 all-reduce.2.cloned.1.call-start
  6.5 85.5 %fusion = f32[2048,2560]{1,0:T(8,128)} fusion(bf16[2048,7168]{1,0:T(8,128)(2,1)} %param.4, bf16[7168,2560]{1,0:T(8,128)(2,1)} %param.5), kind=kOutput, calls=%fused_computation.2 | convolution fusion | flops 75161927680 | bytes 87031808 | tf_op jit(solution)/shard_map/dot_general | solution.py:9
  92.1 91.4 %multiply_convert_fusion = bf16[2048,2560]{1,0:T(8,128)(2,1)} fusion(f32[2048,2560]{1,0:T(8,128)} %fusion, bf16[2048,7168]{1,0:T(8,128)(2,1)} %param.4, bf16[7168,2560]{1,0:T(8,128)(2,1)} %param.6), kind=kOutput, calls=%fused_computation.1 | convolution fusion | flops 75193384960 | bytes 97517568 | tf_op jit(solution)/shard_map/dot_general | solution.py:10
  183.4 85.1 %convolution_convert_fusion = bf16[2048,7168]{1,0:T(8,128)(2,1)} fusion(bf16[2048,2560]{1,0:T(8,128)(2,1)} %multiply_convert_fusion, bf16[2560,7168]{1,0:T(8,128)(2,1)} %param.7), kind=kOutput, calls=%fused_computation | convolution fusion | flops 75176607744 | bytes 76546048 | tf_op jit(solution)/shard_map/dot_general | solution.py:12
  268.6 0.0 all-reduce.2.cloned.1.call-update
  268.6 572.0 %all-reduce.2.cloned.1.call-done = bf16[2048,7168]{1,0:T(8,128)(2,1)} async-done(((bf16[2048,7168]{1,0:T(8,128)(2,1)}), bf16[2048,7168]{1,0:T(8,128)(2,1)}) %all-reduce.2.cloned.1.call-update) | async-done | bytes 29360144 | tf_op jit(solution)/shard_map/psum | solution.py:13
  840.6 20.1 %copy.6 = bf16[2048,7168]{1,0:T(8,128)(2,1)} copy(bf16[2048,7168]{1,0:T(8,128)(2,1)} %all-reduce.2.cloned.1.call-done) | data formatting | bytes 58720256
Async XLA Ops:
  6.5 834.0 %all-reduce.2.cloned.1.call-start = ((), (), s32[]{:S(2)}) async-start(), calls=%async_computation | async-start | bytes 58720256 | tf_op jit(solution)/shard_map/psum | solution.py:13
Sparse Core Ops, SparseCore 0:
  268.7 571.8 all-reduce.1
where the time goes:
time: 868 us
  waiting for transfers between devices  572 us (66%)
  matrix products  262 us (30%)
  local copies, waits for them, and re-layouts  20.1 us (2%)
  between operations  13.4 us (2%)
    psum x1, waiting for transfers between devices, step(): return lax.psum(term, 'tp')  572 us
    dot_general x1, matrix products, step(): up = jnp.dot(x, w_up, preferred_element_type=jnp.float32)  91.4 us
    dot_general x1, matrix products, step(): gate = jnp.dot(x, w_gate, preferred_element_type=jnp.float32)  85.5 us
    dot_general x1, matrix products, step(): jnp.dot(hidden, w_down, preferred_element_type=jnp.float32)  85.1 us
    unnamed x1, local copies, waits for them, and re-layouts  20.1 us
  transfers between devices with their start and end apart: 1, of which 1 were waited for; matrix products, arithmetic and copies ran while one was open for 0% of the time, Pallas kernels for 0%

commit v1 on v0

v1 whole, which is shorter than its diff:
```python
import functools

import jax
import jax.numpy as jnp
from jax import lax
from jax.experimental import pallas as pl
from jax.experimental.pallas import tpu as pltpu
from jax.sharding import PartitionSpec as P

MESH = pl.DeviceIdType.MESH
R = 512
TF = 256
TN = 512
KD = 6
KH = 14
KM = 6
KY = 6
LAG_Y = 2
LAG_O = 6


def kernel(chunks, nf, nt, x_hbm, wg_hbm, wu_hbm, wd_hbm, y_hbm,
           xb, wgb, wub, hid, wdb, sb, d1s, d1r, snd, h1r, h2r, yb,
           x_sem, w_sem, wd_sem, d1_ss, d1_rs, snd_ss, h1_rs, h2_rs, yl_sem, y3_ss, y3_rs, y2_ss, y2_rs,
           cr_d1, cr_h1, cr_h2):
    half = R // 2
    total = chunks * nt
    me = lax.axis_index("tp")
    core = lax.rem(me, 2)
    z = me // 2
    partner = me + 1 - 2 * core
    nbr = (z + 1 - 2 * lax.rem(z, 2)) * 2 + core
    mid = (3 - z) * 2 + core
    inner = jnp.logical_or(z == 1, z == 2)
    outer = jnp.logical_not(inner)

    barrier = pltpu.get_barrier_semaphore()
    pl.semaphore_signal(barrier, inc=1, device_id={"tp": partner}, device_id_type=MESH)
    pl.semaphore_signal(barrier, inc=1, device_id={"tp": nbr}, device_id_type=MESH)

    @pl.when(inner)
    def _():
        pl.semaphore_signal(barrier, inc=1, device_id={"tp": mid}, device_id_type=MESH)
        pl.semaphore_wait(barrier, 3)

    @pl.when(outer)
    def _():
        pl.semaphore_wait(barrier, 2)

    def x_copy(c):
        return pltpu.make_async_copy(x_hbm.at[pl.ds(pl.multiple_of(c * R, R), R), :], xb, x_sem)

    def gu_copies(i, slot):
        cols = pl.ds(pl.multiple_of(i * TF, TF), TF)
        return (
            pltpu.make_async_copy(wg_hbm.at[:, cols], wgb.at[slot], w_sem.at[0, slot]),
            pltpu.make_async_copy(wu_hbm.at[:, cols], wub.at[slot], w_sem.at[1, slot]),
        )

    def wd_copy(j, slot):
        cols = pl.ds(pl.multiple_of(j * TN, TN), TN)
        return pltpu.make_async_copy(wd_hbm.at[:, cols], wdb.at[slot], wd_sem.at[slot])

    def region(p, which):
        row = (p // nt) * R + which * half
        return (
            pl.ds(pl.multiple_of(row, half), half),
            pl.ds(pl.multiple_of(lax.rem(p, nt) * TN, TN), TN),
        )

    def remote(src, dst, ss, rs, to):
        return pltpu.make_async_remote_copy(
            src_ref=src, dst_ref=dst, send_sem=ss, recv_sem=rs,
            device_id={"tp": to}, device_id_type=MESH)

    def d1_copy(p):
        k = lax.rem(p, KD)
        return remote(d1s.at[k], d1r.at[k], d1_ss.at[k], d1_rs.at[k], partner)

    def h1_copy(p):
        k = lax.rem(p, KH)
        return remote(snd.at[k], h1r.at[k], snd_ss.at[k], h1_rs.at[k], nbr)

    def h2_copy(p):
        k, m = lax.rem(p, KH), lax.rem(p, KM)
        return remote(snd.at[k], h2r.at[m], snd_ss.at[k], h2_rs.at[m], mid)

    def y_local(p):
        k = lax.rem(p, KY)
        return pltpu.make_async_copy(yb.at[k], y_hbm.at[region(p, core)], yl_sem.at[k])

    def y_out(p):
        k = lax.rem(p, KY)
        return remote(yb.at[k], y_hbm.at[region(p, core)], y3_ss.at[k], y3_rs.at[p], nbr)

    def y_pair(p):
        k = lax.rem(p, KY)
        return remote(yb.at[k], y_hbm.at[region(p, core)], y2_ss.at[p], y2_rs.at[p], partner)

    def y_free(p):
        y_local(p).wait()
        y_out(p).wait_send()
        y_pair(p).wait_send()

    def forward_copy(p):
        at = region(p, core)
        return remote(y_hbm.at[at], y_hbm.at[at], y2_ss.at[p], y2_rs.at[p], partner)

    def produce(p, slot):
        acc = jnp.dot(hid[...], wdb[slot], preferred_element_type=jnp.float32)
        k, s = lax.rem(p, KD), lax.rem(p, KH)

        @pl.when(p >= KD)
        def _():
            d1_copy(p - KD).wait_send()
            pl.semaphore_wait(cr_d1, 1)

        @pl.when(core == 0)
        def _():
            sb[s] = acc[:half]
            d1s[k] = acc[half:].astype(jnp.bfloat16)

        @pl.when(core == 1)
        def _():
            sb[s] = acc[half:]
            d1s[k] = acc[:half].astype(jnp.bfloat16)

        d1_copy(p).start()

    def chip_sum(p):
        k, s = lax.rem(p, KD), lax.rem(p, KH)
        d1_copy(p).wait_recv()

        @pl.when(inner)
        def _():
            sb[s] = sb[s] + d1r[k].astype(jnp.float32)

        @pl.when(outer)
        def _():
            @pl.when(p >= KH)
            def _():
                h1_copy(p - KH).wait_send()
                pl.semaphore_wait(cr_h1, 1)

            snd[s] = (sb[s] + d1r[k].astype(jnp.float32)).astype(jnp.bfloat16)
            h1_copy(p).start()

        @pl.when(p < total - KD)
        def _():
            pl.semaphore_signal(cr_d1, inc=1, device_id={"tp": partner}, device_id_type=MESH)

    def line_sum(p):
        s = lax.rem(p, KH)
        h1_copy(p).wait_recv()
        snd[s] = (sb[s] + h1r[s].astype(jnp.float32)).astype(jnp.bfloat16)

        @pl.when(p < total - KH)
        def _():
            pl.semaphore_signal(cr_h1, inc=1, device_id={"tp": nbr}, device_id_type=MESH)

        @pl.when(p >= KM)
        def _():
            pl.semaphore_wait(cr_h2, 1)

        h2_copy(p).start()

    def finish(p):
        s, m, k = lax.rem(p, KH), lax.rem(p, KM), lax.rem(p, KY)

        @pl.when(p >= KY)
        def _():
            y_free(p - KY)

        h2_copy(p).wait_recv()
        yb[k] = (snd[s].astype(jnp.float32) + h2r[m].astype(jnp.float32)).astype(jnp.bfloat16)
        h2_copy(p).wait_send()

        @pl.when(p < total - KM)
        def _():
            pl.semaphore_signal(cr_h2, inc=1, device_id={"tp": mid}, device_id_type=MESH)

        y_out(p).start()
        y_pair(p).start()
        y_local(p).start()

    def forward(p):
        y_out(p).wait_recv()
        forward_copy(p).start()

    def tick(p):
        @pl.when(inner)
        def _():
            line_sum(p)

            @pl.when(p >= LAG_Y)
            def _():
                finish(p - LAG_Y)

        @pl.when(jnp.logical_and(outer, p >= LAG_O))
        def _():
            forward(p - LAG_O)

    early = 3
    x_copy(0).start()
    for copy in gu_copies(0, 0):
        copy.start()

    def chunk(c, carry):
        base = c * nt
        x_copy(c).wait()

        def gate_up(i, carry):
            slot = lax.rem(i, 2)

            @pl.when(i + 1 < nf)
            def _():
                for copy in gu_copies(i + 1, 1 - slot):
                    copy.start()

            @pl.when(i == nf - 1)
            def _():
                wd_copy(0, 0).start()

            for copy in gu_copies(i, slot):
                copy.wait()
            gate = jnp.dot(xb[...], wgb[slot], preferred_element_type=jnp.float32)
            up = jnp.dot(xb[...], wub[slot], preferred_element_type=jnp.float32)
            hid[:, pl.ds(pl.multiple_of(i * TF, TF), TF)] = (jax.nn.silu(gate) * up).astype(jnp.bfloat16)

            @pl.when(c >= 1)
            def _():
                tick(base - nt + early + i)

            return carry

        lax.fori_loop(0, nf, gate_up, 0)

        @pl.when(c + 1 < chunks)
        def _():
            for copy in gu_copies(0, 0):
                copy.start()

        def down(j, carry):
            p = base + j
            slot = lax.rem(j, 2)

            @pl.when(j + 1 < nt)
            def _():
                wd_copy(j + 1, 1 - slot).start()

            @pl.when(jnp.logical_and(j == 1, c + 1 < chunks))
            def _():
                x_copy(c + 1).start()

            wd_copy(j, slot).wait()
            produce(p, slot)

            @pl.when(j >= 2)
            def _():
                chip_sum(p - 2)

            @pl.when(jnp.logical_and(j == 2, c >= 1))
            def _():
                tick(base - 1)

            @pl.when(j == 8)
            def _():
                tick(base)

            @pl.when(j == 11)
            def _():
                tick(base + 1)

            return carry

        lax.fori_loop(0, nt, down, 0)
        chip_sum(base + nt - 2)
        chip_sum(base + nt - 1)
        tick(base + 2)
        return carry

    lax.fori_loop(0, chunks, chunk, 0)

    def drain(p, carry):
        tick(p)
        return carry

    lax.fori_loop(total - nt + early, total, drain, 0)

    @pl.when(inner)
    def _():
        for p in range(total - LAG_Y, total):
            finish(p)

        def done(p, carry):
            y_free(p)
            return carry

        lax.fori_loop(total - KY, total, done, 0)

    @pl.when(outer)
    def _():
        def late(p, carry):
            forward(p)
            return carry

        lax.fori_loop(total - LAG_O, total, late, 0)

        def sent(p, carry):
            forward_copy(p).wait_send()
            return carry

        lax.fori_loop(0, total, sent, 0)

        def gone(p, carry):
            h1_copy(p).wait_send()
            return carry

        lax.fori_loop(total - KH, total, gone, 0)

    def drained(p, carry):
        d1_copy(p).wait_send()
        return carry

    lax.fori_loop(total - KD, total, drained, 0)

    def arrived(p, carry):
        at = region(p, 1 - core)
        remote(y_hbm.at[at], y_hbm.at[at], y2_ss.at[p], y2_rs.at[p], partner).wait_recv()
        return carry

    lax.fori_loop(0, total, arrived, 0)


def solution(mesh):
    def step(x, w_gate, w_up, w_down):
        rows, d = x.shape
        f = w_gate.shape[1]
        chunks, nf, nt = rows // R, f // TF, d // TN
        total = chunks * nt
        any_ = pl.BlockSpec(memory_space=pl.ANY)
        bf16, dma = jnp.bfloat16, pltpu.SemaphoreType.DMA
        return pl.pallas_call(
            functools.partial(kernel, chunks, nf, nt),
            out_shape=jax.ShapeDtypeStruct((rows, d), bf16),
            in_specs=[any_] * 4,
            out_specs=any_,
            scratch_shapes=[
                pltpu.VMEM((R, d), bf16),
                pltpu.VMEM((2, d, TF), bf16),
                pltpu.VMEM((2, d, TF), bf16),
                pltpu.VMEM((R, f), bf16),
                pltpu.VMEM((2, f, TN), bf16),
                pltpu.VMEM((KH, R // 2, TN), jnp.float32),
                pltpu.VMEM((KD, R // 2, TN), bf16),
                pltpu.VMEM((KD, R // 2, TN), bf16),
                pltpu.VMEM((KH, R // 2, TN), bf16),
                pltpu.VMEM((KH, R // 2, TN), bf16),
                pltpu.VMEM((KM, R // 2, TN), bf16),
                pltpu.VMEM((KY, R // 2, TN), bf16),
                dma, dma((2, 2)), dma((2,)),
                dma((KD,)), dma((KD,)), dma((KH,)), dma((KH,)), dma((KM,)),
                dma((KY,)), dma((KY,)), dma((total,)), dma((total,)), dma((total,)),
                pltpu.SemaphoreType.REGULAR, pltpu.SemaphoreType.REGULAR, pltpu.SemaphoreType.REGULAR,
            ],
            compiler_params=pltpu.CompilerParams(
                collective_id=0, has_side_effects=True, vmem_limit_bytes=67043328),
        )(x, w_gate, w_up, w_down)

    return jax.shard_map(
        step,
        mesh=mesh,
        in_specs=(P("dp", None), P(None, "tp"), P(None, "tp"), P("tp", None)),
        out_specs=P("dp", None),
        check_vma=False,
    )
```

time: 868 us -> 428 us (0.49)
  waiting for transfers between devices: 572 us -> 0 us
  Pallas kernels: 0 us -> 406 us
  matrix products: 262 us -> 0 us
  between operations: 13.4 us -> 0.01 us
    psum x1 -> x0, waiting for transfers between devices: 572 us -> none  [step(): return lax.psum(term, 'tp')]
    pallas_call x0 -> x1, Pallas kernels: none -> 406 us  [step(): pl.pallas_call(functools.partial(kernel, chunks, nf, nt), out_shape=jax.S...]
    dot_general x3 -> x0, matrix products: 262 us -> none  [the longest x1 91.4 us: step(): up = jnp.dot(x, w_up, preferred_element_type=jnp.float32)]
  transfers between devices with their start and end apart: 1 -> 0, of which waited for: 1 -> 0; matrix products, arithmetic and copies ran while one was open for 0% -> 0% of each run, Pallas kernels for 0% -> 0%
where the time goes in v1:
time: 428 us; the launch traced here: 426 us
  Pallas kernels  406 us (95%)
  local copies, waits for them, and re-layouts  20.2 us (5%)
    pallas_call x1, Pallas kernels, step(): pl.pallas_call(functools.partial(kernel, chunks, nf, nt), out_shape=jax.S...  406 us
    unnamed x1, local copies, waits for them, and re-layouts  20.2 us

profile of v1, /device:TPU:0, one launch (start us, length us, event | category | flops | bytes accessed | tf_op | source)
XLA Modules:
  0.0 426.1 jit_solution(8685170855731089156)
XLA Ops:
  0.0 405.9 %shard_map.46 = bf16[2048,7168]{1,0:T(8,128)(2,1)} custom-call(bf16[2048,7168]{1,0:T(8,128)(2,1)} %x_hbm.1, bf16[7168,2560]{1,0:T(8,128)(2,1)} %wg_hbm.1, bf16[7168,2560]{1,0:T(8,128)(2,1)} %wu_hbm.1, bf16[2560,7168]{1,0:T(8,128)(2,1)} %wd_hbm.1), custom_call_target="tpu_custom_call" | custom-call | tf_op jit(solution)/shard_map/pallas_call | solution.py:343
  405.9 20.2 %copy.6 = bf16[2048,7168]{1,0:T(8,128)(2,1)} copy(bf16[2048,7168]{1,0:T(8,128)(2,1)} %shard_map.46) | data formatting | bytes 58720256

commit v2 on v0

v2 whole, which is shorter than its diff:
```python
import functools

import jax
import jax.numpy as jnp
from jax import lax
from jax.experimental import pallas as pl
from jax.experimental.pallas import tpu as pltpu
from jax.sharding import PartitionSpec as P

MESH = pl.DeviceIdType.MESH
ROWS = (384, 480, 512, 480, 192)
EARLY = (3, 4, 4, 5, 0)
OWN_AT = ((7, 3), (5, 2), (5, 2), (4, 2), (0, 1))
UNDER = (0, 10, 10, 10, 5)
LATE_AT = ((0, 1), (2, 3), (2, 3), (4, 1), (4, 1))
TF = 256
TN = 512
KD = 5
KS = 6
NW = 3
ND = 2
LAG_Y = 2


def kernel(nf, nt, x_hbm, wg_hbm, wu_hbm, wd_hbm, y_hbm,
           xb, wgb, wub, hid, wdb, sb, d1s, d1r, snd, h1r, h2r, yb,
           x_sem, w_sem, wd_sem, d1_ss, d1_rs, snd_ss, h1_rs, h2_rs, yl_sem, y3_ss, y3_rs, y2_ss, y2_rs,
           cr_d1, cr_h1, cr_h2):
    last = len(ROWS) - 1
    first = [sum(ROWS[:c]) for c in range(last + 1)]
    me = lax.axis_index("tp")
    core = lax.rem(me, 2)
    z = me // 2
    partner = me + 1 - 2 * core
    nbr = (z + 1 - 2 * lax.rem(z, 2)) * 2 + core
    mid = (3 - z) * 2 + core
    inner = jnp.logical_or(z == 1, z == 2)
    outer = jnp.logical_not(inner)

    def x_copy(c):
        return pltpu.make_async_copy(
            x_hbm.at[pl.ds(first[c], ROWS[c]), :], xb.at[pl.ds(0, ROWS[c]), :], x_sem)

    def gu_copies(i):
        slot = lax.rem(i, NW)
        cols = pl.ds(pl.multiple_of(i * TF, TF), TF)
        return (
            pltpu.make_async_copy(wg_hbm.at[:, cols], wgb.at[slot], w_sem.at[0, slot]),
            pltpu.make_async_copy(wu_hbm.at[:, cols], wub.at[slot], w_sem.at[1, slot]),
        )

    def wd_copy(j):
        slot = lax.rem(j, ND)
        cols = pl.ds(pl.multiple_of(j * TN, TN), TN)
        return pltpu.make_async_copy(wd_hbm.at[:, cols], wdb.at[slot], wd_sem.at[slot])

    def part(ref, c, k):
        return ref.at[k, pl.ds(0, ROWS[c] // 2), :]

    def region(c, j, which):
        half = ROWS[c] // 2
        return (
            pl.ds(pl.multiple_of(first[c] + which * half, 16), half),
            pl.ds(pl.multiple_of(j * TN, TN), TN),
        )

    def remote(src, dst, ss, rs, to):
        return pltpu.make_async_remote_copy(
            src_ref=src, dst_ref=dst, send_sem=ss, recv_sem=rs,
            device_id={"tp": to}, device_id_type=MESH)

    def signal(sem, to):
        pl.semaphore_signal(sem, inc=1, device_id={"tp": to}, device_id_type=MESH)

    def d1_copy(c, j):
        k = lax.rem(c * nt + j, KD)
        return remote(part(d1s, c, k), part(d1r, c, k), d1_ss.at[k], d1_rs.at[k], partner)

    def h1_copy(c, j):
        return remote(part(snd, c, j), part(h1r, c, j), snd_ss.at[j], h1_rs.at[j], nbr)

    def h2_copy(c, j):
        k = lax.rem(c * nt + j, KS)
        return remote(part(snd, c, j), part(h2r, c, k), snd_ss.at[j], h2_rs.at[k], mid)

    def y_local(c, j):
        k = lax.rem(c * nt + j, KS)
        return pltpu.make_async_copy(part(yb, c, k), y_hbm.at[region(c, j, core)], yl_sem.at[k])

    def y_out(c, j):
        k, p = lax.rem(c * nt + j, KS), c * nt + j
        return remote(part(yb, c, k), y_hbm.at[region(c, j, core)], y3_ss.at[k], y3_rs.at[p], nbr)

    def y_pair(c, j):
        k, p = lax.rem(c * nt + j, KS), c * nt + j
        return remote(part(yb, c, k), y_hbm.at[region(c, j, core)], y2_ss.at[p], y2_rs.at[p], partner)

    def y_free(c, j):
        y_local(c, j).wait()
        y_out(c, j).wait_send()
        y_pair(c, j).wait_send()

    def forward_copy(c, j, which):
        p, at = c * nt + j, region(c, j, which)
        return remote(y_hbm.at[at], y_hbm.at[at], y2_ss.at[p], y2_rs.at[p], partner)

    def before(c, j, lag, act):
        if isinstance(j, int):
            if j >= lag:
                act(c, j - lag)
            elif c >= 1:
                act(c - 1, j - lag + nt)
            return

        @pl.when(j >= lag)
        def _():
            act(c, j - lag)

        if c >= 1:
            @pl.when(j < lag)
            def _():
                act(c - 1, j - lag + nt)

    def unless_last(c, j, slots, act):
        if c < last:
            act()
        elif isinstance(j, int):
            if j < nt - slots:
                act()
        else:
            @pl.when(j < nt - slots)
            def _():
                act()

    def produce(c, j):
        half = ROWS[c] // 2
        acc = jnp.dot(hid[pl.ds(0, ROWS[c]), :], wdb[lax.rem(j, ND)], preferred_element_type=jnp.float32)
        k = lax.rem(c * nt + j, KD)

        def free(c, j):
            d1_copy(c, j).wait_send()
            pl.semaphore_wait(cr_d1, 1)

        before(c, j, KD, free)

        @pl.when(core == 0)
        def _():
            sb[j, pl.ds(0, half), :] = acc[:half]
            d1s[k, pl.ds(0, half), :] = acc[half:].astype(jnp.bfloat16)

        @pl.when(core == 1)
        def _():
            sb[j, pl.ds(0, half), :] = acc[half:]
            d1s[k, pl.ds(0, half), :] = acc[:half].astype(jnp.bfloat16)

        d1_copy(c, j).start()

    def chip_sum(c, j):
        half = ROWS[c] // 2
        k = lax.rem(c * nt + j, KD)
        d1_copy(c, j).wait_recv()

        @pl.when(inner)
        def _():
            sb[j, pl.ds(0, half), :] = sb[j, pl.ds(0, half), :] + d1r[k, pl.ds(0, half), :].astype(jnp.float32)

        @pl.when(outer)
        def _():
            if c >= 1:
                h1_copy(c - 1, j).wait_send()
                pl.semaphore_wait(cr_h1, 1)
            total = sb[j, pl.ds(0, half), :] + d1r[k, pl.ds(0, half), :].astype(jnp.float32)
            snd[j, pl.ds(0, half), :] = total.astype(jnp.bfloat16)
            h1_copy(c, j).start()

        unless_last(c, j, KD, lambda: signal(cr_d1, partner))

    def line_sum(c, j):
        half = ROWS[c] // 2
        h1_copy(c, j).wait_recv()
        total = sb[j, pl.ds(0, half), :] + h1r[j, pl.ds(0, half), :].astype(jnp.float32)
        snd[j, pl.ds(0, half), :] = total.astype(jnp.bfloat16)
        unless_last(c, j, nt, lambda: signal(cr_h1, nbr))
        before(c, j, KS, lambda c, j: pl.semaphore_wait(cr_h2, 1))
        h2_copy(c, j).start()

    def finish(c, j):
        half = ROWS[c] // 2
        k = lax.rem(c * nt + j, KS)
        before(c, j, KS, y_free)
        h2_copy(c, j).wait_recv()
        total = snd[j, pl.ds(0, half), :].astype(jnp.float32) + h2r[k, pl.ds(0, half), :].astype(jnp.float32)
        yb[k, pl.ds(0, half), :] = total.astype(jnp.bfloat16)
        y_out(c, j).start()
        y_pair(c, j).start()
        y_local(c, j).start()
        h2_copy(c, j).wait_send()
        unless_last(c, j, KS, lambda: signal(cr_h2, mid))

    def forward(c, j):
        y_out(c, j).wait_recv()
        forward_copy(c, j, core).start()

    def tick(c, j):
        @pl.when(inner)
        def _():
            line_sum(c, j)
            before(c, j, LAG_Y, finish)

        @pl.when(outer)
        def _():
            if c >= 1:
                forward(c - 1, j)

    def loop(lo, hi, body):
        def step(i, carry):
            body(i)
            return carry

        lax.fori_loop(lo, hi, step, 0)

    x_copy(0).start()
    for i in range(2):
        for copy in gu_copies(i):
            copy.start()

    barrier = pltpu.get_barrier_semaphore()
    signal(barrier, partner)
    signal(barrier, nbr)

    @pl.when(inner)
    def _():
        signal(barrier, mid)
        pl.semaphore_wait(barrier, 3)

    @pl.when(outer)
    def _():
        pl.semaphore_wait(barrier, 2)

    for c in range(last + 1):
        x_copy(c).wait()
        under = UNDER[c]
        late = nt - EARLY[c - 1] - under if c >= 1 else 0

        def gate_up(i):
            @pl.when(i + 2 < nf)
            def _():
                for copy in gu_copies(i + 2):
                    copy.start()

            @pl.when(i == nf - 1)
            def _():
                wd_copy(0).start()

            for copy in gu_copies(i):
                copy.wait()
            slot = lax.rem(i, NW)
            x = xb[pl.ds(0, ROWS[c]), :]
            gate = jnp.dot(x, wgb[slot], preferred_element_type=jnp.float32)
            up = jnp.dot(x, wub[slot], preferred_element_type=jnp.float32)
            cols = pl.ds(pl.multiple_of(i * TF, TF), TF)
            hid[pl.ds(0, ROWS[c]), cols] = (jax.nn.silu(gate) * up).astype(jnp.bfloat16)
            if under:
                at = EARLY[c - 1]
                loop(at + (i * under) // nf, at + ((i + 1) * under) // nf, lambda j: tick(c - 1, j))

        loop(0, nf, gate_up)

        def down(j):
            @pl.when(j + 1 < nt)
            def _():
                wd_copy(j + 1).start()

            if c < last:
                @pl.when(j == 4)
                def _():
                    x_copy(c + 1).start()

                for i in range(2):
                    @pl.when(j == 2 + 4 * i)
                    def _():
                        for copy in gu_copies(i):
                            copy.start()

            wd_copy(j).wait()
            produce(c, j)

            @pl.when(j >= 2)
            def _():
                chip_sum(c, j - 2)

            def spaced(at, count, act):
                start, gap = at

                @pl.when(jnp.logical_and(
                    jnp.logical_and(j >= start, j <= start + (count - 1) * gap), lax.rem(j - start + gap * nt, gap) == 0))
                def _():
                    act((j - start) // gap)

            if late:
                spaced(LATE_AT[c], late, lambda k: tick(c - 1, nt - late + k))
            if EARLY[c]:
                spaced(OWN_AT[c], EARLY[c], lambda k: tick(c, k))

        loop(0, nt, down)
        chip_sum(c, nt - 2)
        chip_sum(c, nt - 1)

    loop(EARLY[last], nt, lambda j: tick(last, j))

    @pl.when(inner)
    def _():
        loop(nt - LAG_Y, nt, lambda j: finish(last, j))
        loop(nt - KS, nt, lambda j: y_free(last, j))

    @pl.when(outer)
    def _():
        loop(0, nt, lambda j: forward(last, j))
        for c in range(last + 1):
            loop(0, nt, lambda j: forward_copy(c, j, core).wait_send())
        loop(0, nt, lambda j: h1_copy(last, j).wait_send())

    loop(nt - KD, nt, lambda j: d1_copy(last, j).wait_send())
    for c in range(last + 1):
        loop(0, nt, lambda j: forward_copy(c, j, 1 - core).wait_recv())


def solution(mesh):
    def step(x, w_gate, w_up, w_down):
        rows, d = x.shape
        f = w_gate.shape[1]
        nf, nt = f // TF, d // TN
        total = len(ROWS) * nt
        top = max(ROWS)
        any_ = pl.BlockSpec(memory_space=pl.ANY)
        bf16, dma, regular = jnp.bfloat16, pltpu.SemaphoreType.DMA, pltpu.SemaphoreType.REGULAR
        return pl.pallas_call(
            functools.partial(kernel, nf, nt),
            out_shape=jax.ShapeDtypeStruct((rows, d), bf16),
            in_specs=[any_] * 4,
            out_specs=any_,
            scratch_shapes=[
                pltpu.VMEM((top, d), bf16),
                pltpu.VMEM((NW, d, TF), bf16),
                pltpu.VMEM((NW, d, TF), bf16),
                pltpu.VMEM((top, f), bf16),
                pltpu.VMEM((ND, f, TN), bf16),
                pltpu.VMEM((nt, top // 2, TN), jnp.float32),
                pltpu.VMEM((KD, top // 2, TN), bf16),
                pltpu.VMEM((KD, top // 2, TN), bf16),
                pltpu.VMEM((nt, top // 2, TN), bf16),
                pltpu.VMEM((nt, top // 2, TN), bf16),
                pltpu.VMEM((KS, top // 2, TN), bf16),
                pltpu.VMEM((KS, top // 2, TN), bf16),
                dma, dma((2, NW)), dma((ND,)),
                dma((KD,)), dma((KD,)), dma((nt,)), dma((nt,)), dma((KS,)),
                dma((KS,)), dma((KS,)), dma((total,)), dma((total,)), dma((total,)),
                regular, regular, regular,
            ],
            compiler_params=pltpu.CompilerParams(
                collective_id=0, has_side_effects=True, vmem_limit_bytes=67043328),
        )(x, w_gate, w_up, w_down)

    return jax.shard_map(
        step,
        mesh=mesh,
        in_specs=(P("dp", None), P(None, "tp"), P(None, "tp"), P("tp", None)),
        out_specs=P("dp", None),
        check_vma=False,
    )
```

time: 868 us -> 419 us (0.48)
  waiting for transfers between devices: 572 us -> 0 us
  Pallas kernels: 0 us -> 398 us
  matrix products: 262 us -> 0 us
  between operations: 13.4 us -> 0.01 us
    psum x1 -> x0, waiting for transfers between devices: 572 us -> none  [step(): return lax.psum(term, 'tp')]
    pallas_call x0 -> x1, Pallas kernels: none -> 398 us  [step(): pl.pallas_call(functools.partial(kernel, nf, nt), out_shape=jax.ShapeDtyp...]
    dot_general x3 -> x0, matrix products: 262 us -> none  [the longest x1 91.4 us: step(): up = jnp.dot(x, w_up, preferred_element_type=jnp.float32)]
  transfers between devices with their start and end apart: 1 -> 0, of which waited for: 1 -> 0; matrix products, arithmetic and copies ran while one was open for 0% -> 0% of each run, Pallas kernels for 0% -> 0%
where the time goes in v2:
time: 419 us; the launch traced here: 418 us
  Pallas kernels  398 us (95%)
  local copies, waits for them, and re-layouts  20.2 us (5%)
    pallas_call x1, Pallas kernels, step(): pl.pallas_call(functools.partial(kernel, nf, nt), out_shape=jax.ShapeDtyp...  398 us
    unnamed x1, local copies, waits for them, and re-layouts  20.2 us

profile of v2, /device:TPU:0, one launch (start us, length us, event | category | flops | bytes accessed | tf_op | source)
XLA Modules:
  0.0 418.0 jit_solution(13233188852685173106)
XLA Ops:
  0.0 397.9 %shard_map.46 = bf16[2048,7168]{1,0:T(8,128)(2,1)} custom-call(bf16[2048,7168]{1,0:T(8,128)(2,1)} %x_hbm.1, bf16[7168,2560]{1,0:T(8,128)(2,1)} %wg_hbm.1, bf16[7168,2560]{1,0:T(8,128)(2,1)} %wu_hbm.1, bf16[2560,7168]{1,0:T(8,128)(2,1)} %wd_hbm.1), custom_call_target="tpu_custom_call" | custom-call | tf_op jit(solution)/shard_map/pallas_call | solution.py:337
  397.9 20.2 %copy.6 = bf16[2048,7168]{1,0:T(8,128)(2,1)} copy(bf16[2048,7168]{1,0:T(8,128)(2,1)} %shard_map.46) | data formatting | bytes 58720256

commit v3 on v2

--- a/solution.py
+++ b/solution.py
@@ -8,17 +8,17 @@
 from jax.sharding import PartitionSpec as P
 
 MESH = pl.DeviceIdType.MESH
-ROWS = (384, 480, 512, 480, 192)
+ROWS = (384, 480, 480, 448, 256)
 EARLY = (3, 4, 4, 5, 0)
-OWN_AT = ((7, 3), (5, 2), (5, 2), (4, 2), (0, 1))
-UNDER = (0, 10, 10, 10, 5)
-LATE_AT = ((0, 1), (2, 3), (2, 3), (4, 1), (4, 1))
+OWN_AT = ((5, 4), (4, 3), (4, 3), (4, 2), (0, 1))
+UNDER = (0, 10, 10, 10, 7)
+LATE_AT = ((0, 1), (1, 1), (4, 4), (0, 4), (4, 3))
 TF = 256
 TN = 512
-KD = 5
-KS = 6
+KD = 4
+KS = 5
 NW = 3
-ND = 2
+ND = 3
 LAG_Y = 2
 
 
@@ -248,9 +248,9 @@
                 for copy in gu_copies(i + 2):
                     copy.start()
 
-            @pl.when(i == nf - 1)
-            def _():
-                wd_copy(0).start()
+            @pl.when(i >= nf - 2)
+            def _():
+                wd_copy(i - (nf - 2)).start()
 
             for copy in gu_copies(i):
                 copy.wait()
@@ -267,9 +267,9 @@
         loop(0, nf, gate_up)
 
         def down(j):
-            @pl.when(j + 1 < nt)
-            def _():
-                wd_copy(j + 1).start()
+            @pl.when(j + 2 < nt)
+            def _():
+                wd_copy(j + 2).start()
 
             if c < last:
                 @pl.when(j == 4)

time: 419 us -> 408 us (0.974)
  Pallas kernels: 398 us -> 387 us
    pallas_call x1, Pallas kernels: 398 us -> 387 us  [step(): pl.pallas_call(functools.partial(kernel, nf, nt), out_shape=jax.ShapeDtyp...]
where the time goes in v3:
time: 408 us
  Pallas kernels  387 us (95%)
  local copies, waits for them, and re-layouts  20.2 us (5%)
    pallas_call x1, Pallas kernels, step(): pl.pallas_call(functools.partial(kernel, nf, nt), out_shape=jax.ShapeDtyp...  387 us
    unnamed x1, local copies, waits for them, and re-layouts  20.2 us

profile of v3, /device:TPU:0, one launch (start us, length us, event | category | flops | bytes accessed | tf_op | source)
XLA Modules:
  0.0 407.5 jit_solution(2765991274952855995)
XLA Ops:
  0.0 387.4 %shard_map.46 = bf16[2048,7168]{1,0:T(8,128)(2,1)} custom-call(bf16[2048,7168]{1,0:T(8,128)(2,1)} %x_hbm.1, bf16[7168,2560]{1,0:T(8,128)(2,1)} %wg_hbm.1, bf16[7168,2560]{1,0:T(8,128)(2,1)} %wu_hbm.1, bf16[2560,7168]{1,0:T(8,128)(2,1)} %wd_hbm.1), custom_call_target="tpu_custom_call" | custom-call | tf_op jit(solution)/shard_map/pallas_call | solution.py:337
  387.4 20.2 %copy.6 = bf16[2048,7168]{1,0:T(8,128)(2,1)} copy(bf16[2048,7168]{1,0:T(8,128)(2,1)} %shard_map.46) | data formatting | bytes 58720256
